TPU v7x, 32 devices: a whole 2x2x4 slice. The times are simulated.
32 devices in a mesh: groups: 2 (over y), row: 4 (over z), col: 4 (over x, core).
Axes of the slice: x: 2, y: 2, z: 4, core: 2. Of those that a mesh axis runs over, the one named last changes fastest.
Arguments:
- activations: bfloat16 [768, 4096], P(('groups', 'row'), 'col'), parts along dimension 0, may hold values from -52 to 52
- damping: float32 [8192], P(('groups', 'row')), parts along dimension 0, may hold values from 0.1 to 1
Outputs:
- factor: float32 [8192, 4096], P(('groups', 'row'), 'col'), parts along dimension 0
There are 2 independent parts, one for each index of `groups`. A program takes and returns all parts, laid end to end along the dimension named above; each array names one. Nothing has to cross between parts.
All inputs are finite; a program needn't handle non-finite values.
Results may differ from a plain program's by a relative error of at most 0.0003.
Values may be sent and summed in bfloat16 or wider, within the bound.
A program may use at most 64 MiB of HBM per device.

v0:
```python
import jax
import jax.numpy as jnp
from jax import lax
from jax.sharding import PartitionSpec as P

NB = 256
PANELS = 2
HIGHEST = lax.Precision.HIGHEST


def from_root(shard, axis, root):
    mine = lax.axis_index(axis) == root
    return lax.psum(jnp.where(mine, shard, jnp.zeros_like(shard)), axis)


def on_device(activations, damping):
    local_tokens = activations.shape[0]
    local_width = activations.shape[1]
    grid_size = lax.axis_size("row")
    row_dev = lax.axis_index("row")
    col_dev = lax.axis_index("col")
    columns = lax.all_gather(activations, "row", axis=0, tiled=True)
    mirrored = from_root(columns, "col", row_dev)
    gram_block = lax.dot_general(
        mirrored, columns, (((0,), (0,)), ((), ())), preferred_element_type=jnp.float32
    )
    diagonal_add = jnp.where(row_dev == col_dev, jnp.diag(damping), 0.0)
    matrix = gram_block / (local_tokens * grid_size) + diagonal_add
    local_index = jnp.arange(local_width, dtype=jnp.int32)
    global_rows = row_dev * local_width + local_index
    global_cols = col_dev * local_width + local_index

    def factor_step(panel_index, matrix):
        begin_at = panel_index * NB
        end_at = begin_at + NB
        owner_row = begin_at // local_width
        offset = begin_at - owner_row * local_width
        below = global_rows[:, None] >= end_at
        corner = lax.dynamic_slice(matrix, (offset, offset), (NB, NB))
        corner = lax.psum(jnp.where(row_dev == owner_row, corner, 0.0), "row")
        safe_corner = jnp.where(col_dev == owner_row, corner, jnp.eye(NB, dtype=jnp.float32))
        pivot_block = jnp.linalg.cholesky(safe_corner)
        own_block = lax.dynamic_slice_in_dim(matrix, offset, NB, 1)
        solved = jax.scipy.linalg.solve_triangular(pivot_block, own_block.T, lower=True).T
        row_side = lax.psum(jnp.where(col_dev == owner_row, solved, 0.0), "col")
        trail_rows = jnp.where(below, row_side, 0.0)
        trail_cols = lax.psum(jnp.where(row_dev == col_dev, trail_rows, 0.0), "row")
        trail_colsT = trail_cols.T
        update = jnp.dot(
            trail_rows, trail_colsT, precision=HIGHEST, preferred_element_type=jnp.float32
        )
        matrix = matrix - update
        placed = lax.dynamic_update_slice(trail_rows, pivot_block, (offset, 0))
        panel_rows = jnp.where(row_dev == owner_row, placed, trail_rows)
        written = lax.dynamic_update_slice(matrix, panel_rows, (0, offset))
        matrix = jnp.where(col_dev == owner_row, written, matrix)
        in_block = (global_rows[:, None] >= begin_at) & (global_rows[:, None] < end_at)
        right_side = global_cols[None, :] >= end_at
        return jnp.where(in_block & right_side, 0.0, matrix)

    return lax.fori_loop(0, PANELS, factor_step, matrix)


def solution(mesh):
    in_specs = (P(("groups", "row"), "col"), P(("groups", "row")))
    out_specs = P(("groups", "row"), "col")
    return jax.shard_map(
        on_device, mesh=mesh, in_specs=in_specs, out_specs=out_specs, check_vma=False
    )
```

profile of v0, /device:TPU:0, one launch (start us, length us, event | category | flops | bytes accessed | tf_op | source)
XLA Modules:
  0.0 492.9 jit_solution(14677081952462626796)
XLA Ops:
  6.5 21.5 %all_gather.3 = bf16[384,1024]{1,0:T(8,128)(2,1)S(1)} all-gather(bf16[96,1024]{1,0:T(8,128)(2,1)} %param.4), channel_id=1, replica_groups=mesh['groups'=2,'row'=4,'col'=4] {'row'}, dimensions={0}, use_global_device_ids=true | all-gather | bytes 983040 | tf_op jit(solution)/shard_map/all_gather | solution.py:22
  28.0 0.9 broadcast_select_fusion.2
  29.0 34.5 %all-reduce.6.cloned.1.call-done = bf16[384,1024]{1,0:T(8,128)(2,1)} async-done(((bf16[384,1024]{1,0:T(8,128)(2,1)}), bf16[384,1024]{1,0:T(8,128)(2,1)}) %all-reduce.6.cloned.1.call-update) | async-done | bytes 786448 | tf_op jit(solution)/shard_map/psum | solution.py:13
  63.5 4.4 select_add_fusion
  68.0 5.3 %copy.9 = f32[1024,1024]{0,1:T(8,128)} copy(f32[1024,1024]{1,0:T(8,128)} %select_add_fusion) | data formatting | bytes 8388608
  73.3 407.4 %while.20 = (s32[]{:T(128)}, f32[1024,1024]{0,1:T(8,128)}, s32[]{:T(128)}, s32[]{:T(128)}, pred[]{:T(512)}, /*index=5*/s32[]{:T(128)}, s32[]{:T(128)}, s32[]{:T(...) while((s32[]{:T(128)}, f32[1024,1024]{0,1:T(8,128)}, ...), condition=%wide.region_9.10_spmd.clone, body=%wide.region_1.9_spmd.clone.sunk | while | flops 3881984256 | bytes 53224180 | solution.py:61
  73.3 1.7 dynamic-slice_select_fusion.2
  75.1 1.3 dynamic-slice_bitcast_fusion.2
  76.4 35.7 %all-reduce.8.cloned.1.call-done = f32[256,256]{0,1:T(8,128)} async-done(((f32[256,256]{0,1:T(8,128)}), f32[256,256]{0,1:T(8,128)}) %all-reduce.8.cloned.1.call-update) | async-done | bytes 262160 | tf_op jit(solution)/shard_map/while/body/eval_jaxpr/psum | solution.py:40
  112.1 1.0 convert_select_fusion.2
  113.1 0.1 copy.18
  113.2 1.0 fusion.55
  114.2 11.7 %cholesky.225 = f32[128,128]{1,0:T(8,128)S(1)} custom-call(f32[128,128]{1,0:T(8,128)S(1)} %cholesky.224), custom_call_target="Cholesky" | custom-call | tf_op jit(solution)/shard_map/while/body/eval_jaxpr/jit(cholesky)/cholesky | solution.py:42
  126.0 9.8 %custom-call.49 = f32[1,128,128]{1,2,0:T(8,128)S(1)} custom-call(f32[1,128,128]{2,1,0:T(8,128)S(1)} %get-tuple-element.322), custom_call_target="InvertDiagBlocksLowerTriangular" | custom-call | tf_op jit(solution)/shard_map/while/body/eval_jaxpr/jit(cholesky)/cholesky | solution.py:42
  135.8 0.2 fusion.56
  136.0 0.3 convolution_subtract_fusion.6
  136.3 11.7 %cholesky.227 = f32[128,128]{1,0:T(8,128)S(1)} custom-call(f32[128,128]{1,0:T(8,128)S(1)} %convolution_subtract_fusion.6), custom_call_target="Cholesky" | custom-call | tf_op jit(solution)/shard_map/while/body/eval_jaxpr/jit(cholesky)/cholesky | solution.py:42
  148.1 0.1 copy.20
  148.3 0.7 compare_reduce_fusion.3
  150.4 4.2 while.21
  150.4 0.6 fusion.62
  151.0 1.4 dynamic-slice.21
  152.5 0.6 fusion.62
  153.1 1.4 dynamic-slice.21
  154.6 19.7 %custom-call.51 = f32[2,128,128]{1,2,0:T(8,128)S(1)} custom-call(f32[2,128,128]{2,1,0:T(8,128)S(1)} %get-tuple-element.326), custom_call_target="InvertDiagBlocksLowerTriangular" | custom-call | tf_op jit(solution)/shard_map/while/body/eval_jaxpr/jit(_solve_triangular)/triangular_solve | solution.py:44
  174.3 0.6 fusion.58
  174.9 0.6 convolution_subtract_fusion.7
  175.5 0.6 fusion.59
  176.2 1.0 fusion.60
  177.3 35.3 %all-reduce.10.cloned.1.call-done = f32[1024,256]{0,1:T(8,128)} async-done(((f32[1024,256]{0,1:T(8,128)}), f32[1024,256]{0,1:T(8,128)}) %all-reduce.10.cloned.1.call-update) | async-done | bytes 1048592 | tf_op jit(solution)/shard_map/while/body/eval_jaxpr/psum | solution.py:45
  212.7 2.5 broadcast_select_fusion.5
  215.2 52.5 %all-reduce.12.cloned.1.call-done = f32[1024,256]{0,1:T(8,128)} async-done(((f32[1024,256]{0,1:T(8,128)}), f32[1024,256]{0,1:T(8,128)}) %all-reduce.12.cloned.1.call-update) | async-done | bytes 1048592 | tf_op jit(solution)/shard_map/while/body/eval_jaxpr/psum | solution.py:47
  267.7 7.2 %convolution_subtract_fusion.8 = f32[1024,1024]{0,1:T(8,128)S(1)} fusion(f32[1024,1024]{0,1:T(8,128)} %get-tuple-element.370, f32[1024,256]{0,1:T(8,128)S(1)} %get-tuple-element.327, f32[1024,256]{0,1:T(8,128)} %all-reduce.12.cloned.1.call-done), kind=kOutput, calls=%fused_computation.5.clone.1 | convolution fusion | flops 3222274048 | bytes 10485760 | tf_op jit(solution)/shard_map/while/body/eval_jaxpr/dot_general | solution.py:49
  274.9 0.2 select_dynamic-update-slice_fusion.5
  275.1 2.4 and_select_fusion.2
  277.5 1.7 dynamic-slice_select_fusion.2
  279.3 1.3 dynamic-slice_bitcast_fusion.2
  280.6 34.6 %all-reduce.8.cloned.1.call-done = f32[256,256]{0,1:T(8,128)} async-done(((f32[256,256]{0,1:T(8,128)}), f32[256,256]{0,1:T(8,128)}) %all-reduce.8.cloned.1.call-update) | async-done | bytes 262160 | tf_op jit(solution)/shard_map/while/body/eval_jaxpr/psum | solution.py:40
  315.2 1.0 convert_select_fusion.2
  316.2 0.1 copy.18
  316.4 1.0 fusion.55
  317.4 11.7 %cholesky.225 = f32[128,128]{1,0:T(8,128)S(1)} custom-call(f32[128,128]{1,0:T(8,128)S(1)} %cholesky.224), custom_call_target="Cholesky" | custom-call | tf_op jit(solution)/shard_map/while/body/eval_jaxpr/jit(cholesky)/cholesky | solution.py:42
  329.1 9.8 %custom-call.49 = f32[1,128,128]{1,2,0:T(8,128)S(1)} custom-call(f32[1,128,128]{2,1,0:T(8,128)S(1)} %get-tuple-element.322), custom_call_target="InvertDiagBlocksLowerTriangular" | custom-call | tf_op jit(solution)/shard_map/while/body/eval_jaxpr/jit(cholesky)/cholesky | solution.py:42
  338.9 0.2 fusion.56
  339.2 0.3 convolution_subtract_fusion.6
  339.4 11.7 %cholesky.227 = f32[128,128]{1,0:T(8,128)S(1)} custom-call(f32[128,128]{1,0:T(8,128)S(1)} %convolution_subtract_fusion.6), custom_call_target="Cholesky" | custom-call | tf_op jit(solution)/shard_map/while/body/eval_jaxpr/jit(cholesky)/cholesky | solution.py:42
  351.5 0.7 compare_reduce_fusion.3
  353.6 4.2 while.21
  353.6 0.6 fusion.62
  354.2 1.4 dynamic-slice.21
  355.7 0.6 fusion.62
  356.2 1.4 dynamic-slice.21
  357.7 19.7 %custom-call.51 = f32[2,128,128]{1,2,0:T(8,128)S(1)} custom-call(f32[2,128,128]{2,1,0:T(8,128)S(1)} %get-tuple-element.326), custom_call_target="InvertDiagBlocksLowerTriangular" | custom-call | tf_op jit(solution)/shard_map/while/body/eval_jaxpr/jit(_solve_triangular)/triangular_solve | solution.py:44
  377.4 0.6 fusion.58
  378.1 0.6 convolution_subtract_fusion.7
  378.7 0.6 fusion.59
  379.3 1.0 fusion.60
  380.5 35.3 %all-reduce.10.cloned.1.call-done = f32[1024,256]{0,1:T(8,128)} async-done(((f32[1024,256]{0,1:T(8,128)}), f32[1024,256]{0,1:T(8,128)}) %all-reduce.10.cloned.1.call-update) | async-done | bytes 1048592 | tf_op jit(solution)/shard_map/while/body/eval_jaxpr/psum | solution.py:45
  415.8 2.5 broadcast_select_fusion.5
  418.3 52.5 %all-reduce.12.cloned.1.call-done = f32[1024,256]{0,1:T(8,128)} async-done(((f32[1024,256]{0,1:T(8,128)}), f32[1024,256]{0,1:T(8,128)}) %all-reduce.12.cloned.1.call-update) | async-done | bytes 1048592 | tf_op jit(solution)/shard_map/while/body/eval_jaxpr/psum | solution.py:47
  470.8 7.2 %convolution_subtract_fusion.8 = f32[1024,1024]{0,1:T(8,128)S(1)} fusion(f32[1024,1024]{0,1:T(8,128)} %get-tuple-element.370, f32[1024,256]{0,1:T(8,128)S(1)} %get-tuple-element.327, f32[1024,256]{0,1:T(8,128)} %all-reduce.12.cloned.1.call-done), kind=kOutput, calls=%fused_computation.5.clone.1 | convolution fusion | flops 3222274048 | bytes 10485760 | tf_op jit(solution)/shard_map/while/body/eval_jaxpr/dot_general | solution.py:49
  478.1 0.2 select_dynamic-update-slice_fusion.5
  478.3 2.4 and_select_fusion.2
  480.7 5.3 %copy.10 = f32[1024,1024]{1,0:T(8,128)} copy(f32[1024,1024]{0,1:T(8,128)} %get-tuple-element.167) | data formatting | bytes 8388608 | tf_op jit(solution)/shard_map/while | solution.py:61
  (57 shorter events, 1.8 us)
Async XLA Ops:
  6.5 57.0 %all-reduce.6.cloned.1.call-start = ((), (), s32[]{:S(2)}) async-start(), calls=%async_computation | async-start | bytes 1572864 | tf_op jit(solution)/shard_map/psum | solution.py:13
  73.3 38.8 %all-reduce.8.cloned.1.call-start = ((), (), s32[]{:S(2)}) async-start(), calls=%async_computation.1 | async-start | bytes 524288 | tf_op jit(solution)/shard_map/while/body/eval_jaxpr/psum | solution.py:40
  75.0 137.7 %all-reduce.10.cloned.1.call-start = ((), (), s32[]{:S(2)}) async-start(), calls=%async_computation.2 | async-start | bytes 2097152 | tf_op jit(solution)/shard_map/while/body/eval_jaxpr/psum | solution.py:45
  177.2 90.4 %all-reduce.12.cloned.1.call-start = ((), (), s32[]{:S(2)}) async-start(), calls=%async_computation.3 | async-start | bytes 2097152 | tf_op jit(solution)/shard_map/while/body/eval_jaxpr/psum | solution.py:47
  277.5 37.7 %all-reduce.8.cloned.1.call-start = ((), (), s32[]{:S(2)}) async-start(), calls=%async_computation.1 | async-start | bytes 524288 | tf_op jit(solution)/shard_map/while/body/eval_jaxpr/psum | solution.py:40
  279.2 136.6 %all-reduce.10.cloned.1.call-start = ((), (), s32[]{:S(2)}) async-start(), calls=%async_computation.2 | async-start | bytes 2097152 | tf_op jit(solution)/shard_map/while/body/eval_jaxpr/psum | solution.py:45
  380.4 90.4 %all-reduce.12.cloned.1.call-start = ((), (), s32[]{:S(2)}) async-start(), calls=%async_computation.3 | async-start | bytes 2097152 | tf_op jit(solution)/shard_map/while/body/eval_jaxpr/psum | solution.py:47
Sparse Core Ops, SparseCore 0:
  29.1 34.3 all-reduce.5
  76.4 35.5 all-reduce.7
  177.4 35.2 all-reduce.9
  215.3 52.3 all-reduce.11
  280.3 34.8 all-reduce.7
  380.5 35.2 all-reduce.9
  418.4 52.3 all-reduce.11
where the time goes:
time: 494 us; the launch traced here: 493 us
  waiting for transfers between devices  281 us (57%)
  other arithmetic  128 us (26%)
  matrix products  23.5 us (5%)
  local copies, waits for them, and re-layouts  22.5 us (5%)
  blocking collectives  21.5 us (4%)
  between operations  13.4 us (3%)
    psum x2, waiting for transfers between devices, factor_step(): trail_cols = lax.psum(jnp.where(row_dev == col_dev, trail_rows, 0.0), 'row')  105 us
    psum x2, waiting for transfers between devices, factor_step(): row_side = lax.psum(jnp.where(col_dev == owner_row, solved, 0.0), 'col')  70.7 us
    psum x2, waiting for transfers between devices, factor_step(): corner = lax.psum(jnp.where(row_dev == owner_row, corner, 0.0), 'row')  70.3 us
    another operation x12, other arithmetic, factor_step(): pivot_block = jnp.linalg.cholesky(safe_corner)  67.9 us
    another operation x6, other arithmetic, factor_step(): jax.scipy.linalg.solve_triangular(pivot_block, own_block.T, lower=True)  39.4 us
    psum x1, waiting for transfers between devices, from_root(): return lax.psum(jnp.where(mine, shard, jnp.zeros_like(shard)), axis)  34.5 us
    all_gather x1, blocking collectives, on_device(): columns = lax.all_gather(activations, 'row', axis=0, tiled=True)  21.5 us
    dot_general x2, matrix products, factor_step(): jnp.dot(trail_rows, trail_colsT, precision=HIGHEST, preferred_element_typ...  14.3 us
  transfers between devices with their start and end apart: 7, of which 7 were waited for; matrix products, arithmetic and copies ran while one was open for 1% of the time, Pallas kernels for 0%

commit v1 on v0

--- a/solution.py
+++ b/solution.py
@@ -44,7 +44,9 @@
         solved = jax.scipy.linalg.solve_triangular(pivot_block, own_block.T, lower=True).T
         row_side = lax.psum(jnp.where(col_dev == owner_row, solved, 0.0), "col")
         trail_rows = jnp.where(below, row_side, 0.0)
-        trail_cols = lax.psum(jnp.where(row_dev == col_dev, trail_rows, 0.0), "row")
+        trail_cols = jnp.sum(
+            lax.all_gather(jnp.where(row_dev == col_dev, trail_rows, 0.0), "row"), axis=0
+        )
         trail_colsT = trail_cols.T
         update = jnp.dot(
             trail_rows, trail_colsT, precision=HIGHEST, preferred_element_type=jnp.float32

time: 494 us -> 569 us (1.15)
  waiting for transfers between devices: 281 us -> 338 us
  local copies, waits for them, and re-layouts: 22.5 us -> 34.5 us
  other arithmetic: 128 us -> 137 us
    all_gather x0 -> x2, waiting for transfers between devices: none -> 163 us  [factor_step(): lax.all_gather(jnp.where(row_dev == col_dev, trail_rows, 0.0), 'row')]
    psum x2 -> x0, waiting for transfers between devices: 105 us -> none  [factor_step(): trail_cols = lax.psum(jnp.where(row_dev == col_dev, trail_rows, 0.0), 'row')]
    all_gather x0 -> x2, local copies, waits for them, and re-layouts: none -> 12 us  [factor_step(): lax.all_gather(jnp.where(row_dev == col_dev, trail_rows, 0.0), 'row')]
    reduce_sum x0 -> x2, other arithmetic: none -> 9.48 us  [factor_step(): jnp.sum(lax.all_gather(jnp.where(row_dev == col_dev, trail_rows, 0.0), 'r...]
  transfers between devices with their start and end apart: 7 -> 7, of which waited for: 7 -> 7; matrix products, arithmetic and copies ran while one was open for 1% -> 0% of each run, Pallas kernels for 0% -> 0%
where the time goes in v1:
time: 569 us; the launch traced here: 568 us
  waiting for transfers between devices  338 us (59%)
  other arithmetic  137 us (24%)
  local copies, waits for them, and re-layouts  34.5 us (6%)
  blocking collectives  21.5 us (4%)
  matrix products  20 us (4%)
  between operations  13.4 us (2%)
    all_gather x2, waiting for transfers between devices, factor_step(): lax.all_gather(jnp.where(row_dev == col_dev, trail_rows, 0.0), 'row')  163 us
    psum x2, waiting for transfers between devices, factor_step(): row_side = lax.psum(jnp.where(col_dev == owner_row, solved, 0.0), 'col')  70.7 us
    psum x2, waiting for transfers between devices, factor_step(): corner = lax.psum(jnp.where(row_dev == owner_row, corner, 0.0), 'row')  69.5 us
    another operation x12, other arithmetic, factor_step(): pivot_block = jnp.linalg.cholesky(safe_corner)  67.9 us
    another operation x6, other arithmetic, factor_step(): jax.scipy.linalg.solve_triangular(pivot_block, own_block.T, lower=True)  39.4 us
    psum x1, waiting for transfers between devices, from_root(): return lax.psum(jnp.where(mine, shard, jnp.zeros_like(shard)), axis)  34.5 us
    all_gather x1, blocking collectives, on_device(): columns = lax.all_gather(activations, 'row', axis=0, tiled=True)  21.5 us
    all_gather x2, local copies, waits for them, and re-layouts, factor_step(): lax.all_gather(jnp.where(row_dev == col_dev, trail_rows, 0.0), 'row')  12 us
  transfers between devices with their start and end apart: 7, of which 7 were waited for; matrix products, arithmetic and copies ran while one was open for 0% of the time, Pallas kernels for 0%

profile of v1, /device:TPU:0, one launch (start us, length us, event | category | flops | bytes accessed | tf_op | source)
XLA Modules:
  0.0 567.7 jit_solution(234010666290158842)
XLA Ops:
  6.5 21.5 %all_gather.23 = bf16[384,1024]{1,0:T(8,128)(2,1)S(1)} all-gather(bf16[96,1024]{1,0:T(8,128)(2,1)} %param.4), channel_id=1, replica_groups=mesh['groups'=2,'row'=4,'col'=4] {'row'}, dimensions={0}, use_global_device_ids=true | all-gather | bytes 983040 | tf_op jit(solution)/shard_map/all_gather | solution.py:22
  28.0 0.9 broadcast_select_fusion.2
  29.0 34.5 %all-reduce.5.cloned.1.call-done = bf16[384,1024]{1,0:T(8,128)(2,1)} async-done(((bf16[384,1024]{1,0:T(8,128)(2,1)}), bf16[384,1024]{1,0:T(8,128)(2,1)}) %all-reduce.5.cloned.1.call-update) | async-done | bytes 786448 | tf_op jit(solution)/shard_map/psum | solution.py:13
  63.5 4.4 select_add_fusion
  68.0 5.3 copy.17
  73.3 482.2 %while.20 = (s32[]{:T(128)}, f32[1024,1024]{0,1:T(8,128)}, s32[]{:T(128)}, s32[]{:T(128)}, pred[]{:T(512)}, /*index=5*/s32[]{:T(128)}, s32[]{:T(128)}, s32[]{:T(...) while((s32[]{:T(128)}, f32[1024,1024]{0,1:T(8,128)}, ...), condition=%wide.region_9.10_spmd.clone, body=%wide.region_1.9_spmd.clone.sunk | while | flops 3882508544 | bytes 76292872 | solution.py:63
  73.3 1.7 dynamic-slice_select_fusion.2
  75.1 1.3 dynamic-slice_bitcast_fusion.2
  76.4 35.7 %all-reduce.7.cloned.1.call-done = f32[256,256]{0,1:T(8,128)} async-done(((f32[256,256]{0,1:T(8,128)}), f32[256,256]{0,1:T(8,128)}) %all-reduce.7.cloned.1.call-update) | async-done | bytes 262160 | tf_op jit(solution)/shard_map/while/body/eval_jaxpr/psum | solution.py:40
  112.1 1.0 convert_select_fusion.2
  113.2 1.0 fusion.55
  114.2 11.7 %cholesky.225 = f32[128,128]{1,0:T(8,128)S(1)} custom-call(f32[128,128]{1,0:T(8,128)S(1)} %cholesky.224), custom_call_target="Cholesky" | custom-call | tf_op jit(solution)/shard_map/while/body/eval_jaxpr/jit(cholesky)/cholesky | solution.py:42
  126.1 9.8 %custom-call.49 = f32[1,128,128]{1,2,0:T(8,128)S(1)} custom-call(f32[1,128,128]{2,1,0:T(8,128)S(1)} %get-tuple-element.333), custom_call_target="InvertDiagBlocksLowerTriangular" | custom-call | tf_op jit(solution)/shard_map/while/body/eval_jaxpr/jit(cholesky)/cholesky | solution.py:42
  135.9 0.2 fusion.56
  136.2 0.3 convolution_subtract_fusion.6
  136.5 11.7 %cholesky.227 = f32[128,128]{1,0:T(8,128)S(1)} custom-call(f32[128,128]{1,0:T(8,128)S(1)} %convolution_subtract_fusion.6), custom_call_target="Cholesky" | custom-call | tf_op jit(solution)/shard_map/while/body/eval_jaxpr/jit(cholesky)/cholesky | solution.py:42
  148.4 0.6 compare_reduce_fusion.3
  150.4 4.2 while.21
  150.4 0.6 fusion.62
  151.0 1.4 dynamic-slice.21
  152.5 0.6 fusion.62
  153.1 1.4 dynamic-slice.21
  154.6 19.7 %custom-call.51 = f32[2,128,128]{1,2,0:T(8,128)S(1)} custom-call(f32[2,128,128]{2,1,0:T(8,128)S(1)} %get-tuple-element.337), custom_call_target="InvertDiagBlocksLowerTriangular" | custom-call | tf_op jit(solution)/shard_map/while/body/eval_jaxpr/jit(_solve_triangular)/triangular_solve | solution.py:44
  174.3 0.6 fusion.58
  174.9 0.6 convolution_subtract_fusion.7
  175.5 0.6 fusion.59
  176.2 1.0 fusion.60
  177.3 35.3 %all-reduce.9.cloned.1.call-done = f32[1024,256]{0,1:T(8,128)} async-done(((f32[1024,256]{0,1:T(8,128)}), f32[1024,256]{0,1:T(8,128)}) %all-reduce.9.cloned.1.call-update) | async-done | bytes 1048592 | tf_op jit(solution)/shard_map/while/body/eval_jaxpr/psum | solution.py:45
  212.7 2.5 broadcast_select_fusion.5
  215.2 81.3 %all-gather.6.cloned.1.call-done = f32[4096,256]{0,1:T(8,128)} async-done(((f32[1024,256]{0,1:T(8,128)}), f32[4096,256]{0,1:T(8,128)}) %all-gather.6.cloned.1.call-update) | async-done | bytes 4194320 | tf_op jit(solution)/shard_map/while/body/eval_jaxpr/all_gather | solution.py:48
  296.5 6.0 %reshape.113 = f32[4,1024,256]{1,0,2:T(4,128)} reshape(f32[4096,256]{0,1:T(8,128)} %all-gather.6.cloned.1.call-done) | data formatting | bytes 8388608 | tf_op jit(solution)/shard_map/while/body/eval_jaxpr/all_gather | solution.py:48
  302.5 4.7 reduce_sum.18
  307.3 5.4 convolution_subtract_fusion.8
  312.7 0.2 select_dynamic-update-slice_fusion.5
  313.0 2.4 and_select_fusion.2
  315.4 1.7 dynamic-slice_select_fusion.2
  317.1 1.3 dynamic-slice_bitcast_fusion.2
  318.4 33.8 %all-reduce.7.cloned.1.call-done = f32[256,256]{0,1:T(8,128)} async-done(((f32[256,256]{0,1:T(8,128)}), f32[256,256]{0,1:T(8,128)}) %all-reduce.7.cloned.1.call-update) | async-done | bytes 262160 | tf_op jit(solution)/shard_map/while/body/eval_jaxpr/psum | solution.py:40
  352.3 1.0 convert_select_fusion.2
  353.4 1.0 fusion.55
  354.4 11.7 %cholesky.225 = f32[128,128]{1,0:T(8,128)S(1)} custom-call(f32[128,128]{1,0:T(8,128)S(1)} %cholesky.224), custom_call_target="Cholesky" | custom-call | tf_op jit(solution)/shard_map/while/body/eval_jaxpr/jit(cholesky)/cholesky | solution.py:42
  366.3 9.8 %custom-call.49 = f32[1,128,128]{1,2,0:T(8,128)S(1)} custom-call(f32[1,128,128]{2,1,0:T(8,128)S(1)} %get-tuple-element.333), custom_call_target="InvertDiagBlocksLowerTriangular" | custom-call | tf_op jit(solution)/shard_map/while/body/eval_jaxpr/jit(cholesky)/cholesky | solution.py:42
  376.4 0.3 convolution_subtract_fusion.6
  376.7 11.7 %cholesky.227 = f32[128,128]{1,0:T(8,128)S(1)} custom-call(f32[128,128]{1,0:T(8,128)S(1)} %convolution_subtract_fusion.6), custom_call_target="Cholesky" | custom-call | tf_op jit(solution)/shard_map/while/body/eval_jaxpr/jit(cholesky)/cholesky | solution.py:42
  388.6 0.6 compare_reduce_fusion.3
  390.6 4.2 while.21
  390.6 0.6 fusion.62
  391.2 1.4 dynamic-slice.21
  392.7 0.6 fusion.62
  393.3 1.4 dynamic-slice.21
  394.8 19.7 %custom-call.51 = f32[2,128,128]{1,2,0:T(8,128)S(1)} custom-call(f32[2,128,128]{2,1,0:T(8,128)S(1)} %get-tuple-element.337), custom_call_target="InvertDiagBlocksLowerTriangular" | custom-call | tf_op jit(solution)/shard_map/while/body/eval_jaxpr/jit(_solve_triangular)/triangular_solve | solution.py:44
  414.4 0.6 fusion.58
  415.1 0.6 convolution_subtract_fusion.7
  415.7 0.6 fusion.59
  416.4 1.0 fusion.60
  417.5 35.3 %all-reduce.9.cloned.1.call-done = f32[1024,256]{0,1:T(8,128)} async-done(((f32[1024,256]{0,1:T(8,128)}), f32[1024,256]{0,1:T(8,128)}) %all-reduce.9.cloned.1.call-update) | async-done | bytes 1048592 | tf_op jit(solution)/shard_map/while/body/eval_jaxpr/psum | solution.py:45
  452.8 2.5 broadcast_select_fusion.5
  455.3 81.3 %all-gather.6.cloned.1.call-done = f32[4096,256]{0,1:T(8,128)} async-done(((f32[1024,256]{0,1:T(8,128)}), f32[4096,256]{0,1:T(8,128)}) %all-gather.6.cloned.1.call-update) | async-done | bytes 4194320 | tf_op jit(solution)/shard_map/while/body/eval_jaxpr/all_gather | solution.py:48
  536.7 6.0 %reshape.113 = f32[4,1024,256]{1,0,2:T(4,128)} reshape(f32[4096,256]{0,1:T(8,128)} %all-gather.6.cloned.1.call-done) | data formatting | bytes 8388608 | tf_op jit(solution)/shard_map/while/body/eval_jaxpr/all_gather | solution.py:48
  542.7 4.7 reduce_sum.18
  547.5 5.4 convolution_subtract_fusion.8
  552.9 0.2 select_dynamic-update-slice_fusion.5
  553.1 2.4 and_select_fusion.2
  555.6 5.3 copy.18
  (61 shorter events, 2.3 us)
Async XLA Ops:
  6.5 57.0 %all-reduce.5.cloned.1.call-start = ((), (), s32[]{:S(2)}) async-start(), calls=%async_computation | async-start | bytes 1572864 | tf_op jit(solution)/shard_map/psum | solution.py:13
  73.3 38.8 %all-reduce.7.cloned.1.call-start = ((), (), s32[]{:S(2)}) async-start(), calls=%async_computation.1 | async-start | bytes 524288 | tf_op jit(solution)/shard_map/while/body/eval_jaxpr/psum | solution.py:40
  75.0 137.6 %all-reduce.9.cloned.1.call-start = ((), (), s32[]{:S(2)}) async-start(), calls=%async_computation.2 | async-start | bytes 2097152 | tf_op jit(solution)/shard_map/while/body/eval_jaxpr/psum | solution.py:45
  177.2 119.3 %all-gather.6.cloned.1.call-start = ((), (), s32[]{:S(2)}) async-start(), calls=%async_computation.3 | async-start | bytes 5242880 | tf_op jit(solution)/shard_map/while/body/eval_jaxpr/all_gather | solution.py:48
  315.4 36.9 %all-reduce.7.cloned.1.call-start = ((), (), s32[]{:S(2)}) async-start(), calls=%async_computation.1 | async-start | bytes 524288 | tf_op jit(solution)/shard_map/while/body/eval_jaxpr/psum | solution.py:40
  317.1 135.8 %all-reduce.9.cloned.1.call-start = ((), (), s32[]{:S(2)}) async-start(), calls=%async_computation.2 | async-start | bytes 2097152 | tf_op jit(solution)/shard_map/while/body/eval_jaxpr/psum | solution.py:45
  417.4 119.3 %all-gather.6.cloned.1.call-start = ((), (), s32[]{:S(2)}) async-start(), calls=%async_computation.3 | async-start | bytes 5242880 | tf_op jit(solution)/shard_map/while/body/eval_jaxpr/all_gather | solution.py:48
Sparse Core Ops, SparseCore 0:
  29.1 34.3 all-reduce.4
  76.4 35.5 all-reduce.6
  177.4 35.2 all-reduce.8
  215.3 81.2 all-gather.5
  318.2 34.0 all-reduce.6
  417.6 35.2 all-reduce.8
  455.5 81.2 all-gather.5
